TPU v7x, 32 devices: a whole 2x2x4 slice. The times are simulated.
32 devices in a mesh: seq: 16 (over z, y, core), head: 2 (over x).
Axes of the slice: x: 2, y: 2, z: 4, core: 2. Of those that a mesh axis runs over, the one named last changes fastest.
Arguments:
- tokens: bfloat16 [1, 8192, 2048], P(None, 'seq'), may hold values from -6 to 6
- qkv_weight: bfloat16 [2048, 3, 2048], P(None, None, 'head'), may hold values from -1 to 1
- persistent: bfloat16 [2, 128, 2048], P(None, None, 'head'), may hold values from -60 to 60
- rate_weight: float32 [2048], replicated, may hold values from -0.25 to 0.25
- forget_rate: float32 [1, 8192], P(None, 'seq'), may hold values from 9.765625e-07 to 0.0009765625
- momentum_decay: float32 [1], replicated, may hold values from 0.5 to 0.95
- forget_share: float32 [1], replicated, may hold values from 0.05 to 0.5
- memory: float32 [2048, 2, 4096], P('seq', None, 'head'), may hold values from -0.125 to 0.125
- momentum: float32 [2048, 2, 4096], P('seq', None, 'head'), may hold values from -0.0625 to 0.0625
Outputs:
- attended: bfloat16 [1, 8192, 2048], P(None, 'seq', 'head')
- memory_out: float32 [2048, 2, 4096], P('seq', None, 'head')
- momentum_out: float32 [2048, 2, 4096], P('seq', None, 'head')
All inputs are finite; a program needn't handle non-finite values.
Results may differ from a plain program's by a relative error of at most 0.01.
Values may be sent and summed in bfloat16 or wider, within the bound.
A program may use at most 128 MiB of HBM per device.

v0:
```python
import jax
import jax.numpy as jnp
from jax import lax
from jax.sharding import PartitionSpec as P

HEAD_DIM = 128


def entering(value, axis, combine, identity):
    size, mine = (lax.axis_size(axis), lax.axis_index(axis))
    everything = lax.all_gather(value, axis)
    start = jnp.broadcast_to(jnp.asarray(identity, value.dtype), value.shape)

    def hop(k, before):
        at = size - 1 - k
        reached = at > mine
        new = combine(before, everything[at])
        return jnp.where(reached, new, before)

    return lax.fori_loop(0, size, hop, start)


def add_pair(earlier, later):
    return earlier + later


def key_mask(count, persist_count):
    rows_at = jnp.arange(count)[:, None]
    column = jnp.arange(persist_count + 2 * count)[None, :]
    local_pos = jnp.where(
        column < persist_count + count, column - persist_count, column - persist_count - count
    )
    return (column < persist_count) | (local_pos <= rows_at)


def attend_local(query, keys, values, recalled, persistent):
    count = query.shape[0]
    heads_here = query.shape[1] // HEAD_DIM
    persist_count = persistent.shape[1]
    persist_keys = persistent[0].reshape(persist_count, heads_here, HEAD_DIM)
    persist_values = persistent[1].reshape(persist_count, heads_here, HEAD_DIM)
    recall_heads = recalled.reshape(count, heads_here, HEAD_DIM)
    all_keys = jnp.concatenate(
        [persist_keys, recall_heads, keys.reshape(count, heads_here, HEAD_DIM)], axis=0
    )
    all_values = jnp.concatenate(
        [persist_values, recall_heads, values.reshape(count, heads_here, HEAD_DIM)], axis=0
    )
    scores = jnp.einsum(
        "thd,nhd->htn",
        query.reshape(count, heads_here, HEAD_DIM),
        all_keys,
        preferred_element_type=jnp.float32,
    ) * HEAD_DIM ** (-0.5)
    visible = key_mask(count, persist_count)
    scores = jnp.where(visible[None], scores, -1e30)
    largest = jnp.max(scores, axis=2, keepdims=True)
    expo = jnp.exp(scores - largest)
    probs = (expo / jnp.sum(expo, axis=2, keepdims=True)).astype(jnp.bfloat16)
    result = jnp.einsum("htn,nhd->thd", probs, all_values, preferred_element_type=jnp.float32)
    return result.astype(jnp.bfloat16).reshape(count, heads_here * HEAD_DIM)


def memory_forward(query_full, keys_full, first, second):
    stacked = jnp.concatenate([query_full, keys_full], axis=0)
    preact = jnp.dot(stacked, first, preferred_element_type=jnp.float32)
    hidden = jax.nn.silu(preact).astype(jnp.bfloat16)
    partial_out = lax.dot_general(
        hidden, second, (((1,), (1,)), ((), ())), preferred_element_type=jnp.float32
    )
    return (preact, hidden, partial_out)


def reduce_terms(keys_full, errors_full, wdz, whid):
    grad_first = lax.dot_general(
        keys_full, wdz, (((0,), (0,)), ((), ())), preferred_element_type=jnp.float32
    )
    grad_second = lax.dot_general(
        errors_full, whid, (((0,), (0,)), ((), ())), preferred_element_type=jnp.float32
    )
    return lax.psum_scatter(
        jnp.stack([grad_first, grad_second], axis=1).astype(jnp.bfloat16),
        "seq",
        scatter_dimension=0,
        tiled=True,
    ).astype(jnp.float32)


def on_device(
    tokens,
    qkv_weight,
    persistent,
    rate_weight,
    forget_rate,
    momentum_decay,
    forget_share,
    memory,
    momentum,
):
    seg_len = tokens.shape[1]
    width = tokens.shape[2]
    steps_len = lax.axis_size("seq") * seg_len
    lr_scale = 2.0 / (width * steps_len) ** 0.5
    totals = jnp.sum(forget_rate, axis=1)
    later = entering(totals, "seq", add_pair, jnp.zeros_like(totals))
    tail = totals[:, None] - jnp.cumsum(forget_rate, axis=1) + later[:, None]
    weights_low = lax.all_gather(memory.astype(jnp.bfloat16), "seq", axis=0, tiled=True)
    first = weights_low[:, 0, :]
    second = weights_low[:, 1, :]
    inputs = tokens[0]
    proj = jnp.einsum("td,dkf->tkf", inputs, qkv_weight, preferred_element_type=jnp.float32).astype(
        jnp.bfloat16
    )
    query = proj[:, 0]
    keys = proj[:, 1]
    values = proj[:, 2]
    query_full = lax.all_gather(query, "head", axis=1, tiled=True)
    keys_full = lax.all_gather(keys, "head", axis=1, tiled=True)
    preact, hidden, partial_out = memory_forward(query_full, keys_full, first, second)
    summed = lax.psum_scatter(
        partial_out.astype(jnp.bfloat16), "head", scatter_dimension=1, tiled=True
    ).astype(jnp.float32)
    recalled = summed[:seg_len].astype(jnp.bfloat16)
    errors_here = (summed[seg_len:] - values.astype(jnp.float32)).astype(jnp.bfloat16)
    errors_full = lax.all_gather(errors_here, "head", axis=1, tiled=True)
    rate = lr_scale * jax.nn.sigmoid(
        jnp.dot(inputs.astype(jnp.float32), rate_weight, precision=lax.Precision.HIGHEST)
    )
    weight = rate * jnp.exp(-tail[0])
    key_pre = preact[seg_len:]
    key_hidden = hidden[seg_len:]
    sigm = jax.nn.sigmoid(key_pre)
    back = jnp.dot(errors_full, second, preferred_element_type=jnp.float32)
    dpre = back * sigm * (1.0 + key_pre * (1.0 - sigm))
    wdz = (weight[:, None] * dpre).astype(jnp.bfloat16)
    whid = (weight[:, None] * key_hidden.astype(jnp.float32)).astype(jnp.bfloat16)
    attended = attend_local(query, keys, values, recalled, persistent)
    grad = reduce_terms(keys_full, errors_full, wdz, whid)
    results = [attended]
    momentum = momentum_decay[0] * momentum - grad
    memory = (1.0 - forget_share[0]) * memory + momentum
    return (jnp.stack(results, axis=0), memory, momentum)


def solution(mesh):
    placed = (
        P(None, "seq", None),
        P(None, None, "head"),
        P(None, None, "head"),
        P(),
        P(None, "seq"),
        P(),
        P(),
        P("seq", None, "head"),
        P("seq", None, "head"),
    )
    return jax.shard_map(
        on_device,
        mesh=mesh,
        in_specs=placed,
        out_specs=(P(None, "seq", "head"), P("seq", None, "head"), P("seq", None, "head")),
        check_vma=False,
    )
```

profile of v0, /device:TPU:0, one launch (start us, length us, event | category | flops | bytes accessed | tf_op | source)
XLA Modules:
  0.0 597.3 jit_solution(6255151362418320822)
XLA Ops:
  8.8 9.8 %convolution_convert_fusion = bf16[512,3,1024]{2,0,1:T(8,128)(2,1)S(1)} fusion(bf16[2048,3,1024]{2,0,1:T(8,128)(2,1)} %param.12, bf16[1,512,2048]{2,1,0:T(8,128)(2,1)S(1)} %copy-done), kind=kOutput, calls=%fused_computation.35 | convolution fusion | flops 6444023808 | bytes 17825792 | tf_op jit(solution)/shard_map/td,dkf->tkf/dot_general | solution.py:111
  20.2 2.6 fusion.45
  23.6 3.7 copy.51
  27.4 31.4 %all-gather.13.cloned.1.call-done = bf16[512,1,2048]{2,0,1:T(8,128)(2,1)} async-done(((bf16[512,1,1024]{2,0,1:T(8,128)(2,1)}), bf16[512,1,2048]{2,0,1:T(8,128)(2,1)}) %all-gather.13.cloned.1.call-update) | async-done | bytes 2097168 | tf_op jit(solution)/shard_map/all_gather | solution.py:118
  58.8 34.7 %all-gather.11.cloned.1.call-done = bf16[512,1,2048]{2,0,1:T(8,128)(2,1)} async-done(((bf16[512,1,1024]{2,0,1:T(8,128)(2,1)}), bf16[512,1,2048]{2,0,1:T(8,128)(2,1)}) %all-gather.11.cloned.1.call-update) | async-done | bytes 2097168 | tf_op jit(solution)/shard_map/all_gather | solution.py:117
  93.4 128.7 %all-gather.7.cloned.1.call-done = bf16[2048,2,2048]{2,0,1:T(8,128)(2,1)} async-done(((bf16[128,2,2048]{2,0,1:T(8,128)(2,1)}), bf16[2048,2,2048]{2,0,1:T(8,128)(2,1)}) %all-gather.7.cloned.1.call-update) | async-done | bytes 16777232 | tf_op jit(solution)/shard_map/all_gather | solution.py:107
  222.1 16.0 %multiply_convert_fusion = (bf16[1024,2048]{1,0:T(8,128)(2,1)}, f32[1024,2048]{1,0:T(8,128)}) fusion(bf16[2048,2,2048]{2,0,1:T(8,128)(2,1)} %all-gather.7.cloned.1.call-done, bf16[512,2048]{1,0:T(8,128)(2,1)} %bitcast.115, bf16[512,2048]{1,0:T(8,128)(2,1)} %bitcast.116), kind=kOutput, calls=%fused_computation.14 | convolution fusion | flops 8608808960 | bytes 25165824 | tf_op jit(solution)/shard_map/dot_general | solution.py:66
  238.1 12.0 %fusion.10 = bf16[1024,2048]{1,0:T(8,128)(2,1)} fusion(bf16[1024,2048]{1,0:T(8,128)(2,1)} %get-tuple-element.139, bf16[2048,2,2048]{2,0,1:T(8,128)(2,1)S(1)} %copy-done.11), kind=kOutput, calls=%fused_computation.22 | convolution fusion | flops 8592031744 | bytes 16777216 | tf_op jit(solution)/shard_map/dot_general | solution.py:68
  250.7 52.2 %reduce-scatter.3.cloned.1.call-done = bf16[1024,1024]{1,0:T(8,128)(2,1)} async-done(((bf16[1024,2048]{1,0:T(8,128)(2,1)}), bf16[1024,1024]{1,0:T(8,128)(2,1)}) %reduce-scatter.3.cloned.1.call-update) | async-done | bytes 2097168 | tf_op jit(solution)/shard_map/reduce_scatter | solution.py:120
  302.9 2.9 fusion.23
  308.4 33.0 %all-reduce = f32[16]{0:T(128)S(1)} all-reduce(f32[16]{0:T(128)S(1)} %dynamic-update-slice), channel_id=1, replica_groups=mesh['seq'=16,'head'=2] {'seq'}, use_global_device_ids=true, to_apply=%add | all-reduce | flops 16 | bytes 128
  342.1 22.3 %while.15 = (s32[]{:T(128)}, f32[1]{0:T(128)}, s32[]{:T(128)}, f32[16,1]{0,1:T(1,128)S(1)}, s32[]{:T(128)}, /*index=5*/s32[]{:T(128)}, s32[]{:T(128)}, s32[]{:T(128)}) while((s32[]{:T(128)}, f32[1]{0:T(128)}, s32[]{:T(128)}, f32[16,1]{0,1:T(1,128)S(1)}, s32[]{:T(128)}, /*index=5*/s32[]{:T(128)}, s32[]{:T(128)}, s32[]{:T(128)}) %tuple.65), condition=%wide.region_7.8_spmd, body=%wide.region_6.7_spmd.sunk | while | flops 9 | bytes 177 | solution.py:20
  366.7 10.2 %convert_bitcast_fusion = bf16[2048,1,2048]{2,0,1:T(8,128)(2,1)} fusion(bf16[512,2048]{1,0:T(8,128)(2,1)} %all-gather.9.cloned.1.call-done, bf16[1024,2048]{1,0:T(8,128)(2,1)} %get-tuple-element.139, f32[512]{0:T(512)S(1)} %fusion.38), kind=kOutput, calls=%fused_computation.12 | convolution fusion | flops 4302307328 | bytes 12584960 | tf_op jit(solution)/shard_map/dot_general | solution.py:78
  377.0 15.5 %convert_bitcast_fusion.1 = bf16[2048,1,2048]{2,0,1:T(8,128)(2,1)} fusion(bf16[512,1,2048]{2,0,1:T(8,128)(2,1)} %all-gather.13.cloned.1.call-done, f32[1024,2048]{1,0:T(8,128)} %get-tuple-element.140, bf16[512,2048]{1,0:T(8,128)(2,1)} %all-gather.9.cloned.1.call-done, bf16[2048,2,2048]{2,0,1:T(8,128)(2,1)} %all-gather.7.cloned.1.call-done, f32[512]{0:T(512)S(1)} %fusion.38), kind=kOutput, calls=%fused_computation.13 | convolution fusion | flops 8604614656 | bytes 25167872 | tf_op jit(solution)/shard_map/dot_general | solution.py:75
  392.4 13.8 %pad_maximum_fusion = bf16[2048,2,2048]{2,0,1:T(8,128)(2,1)} fusion(bf16[2048,1,2048]{2,0,1:T(8,128)(2,1)} %convert_bitcast_fusion, bf16[2048,1,2048]{2,0,1:T(8,128)(2,1)} %convert_bitcast_fusion.1), kind=kLoop, calls=%fused_computation.7 | loop fusion | flops 8388608 | bytes 33554432 | tf_op jit(solution)/shard_map/stack | solution.py:82
  419.3 2.5 copy.25
  421.7 10.9 %fusion.2 = f32[8,512,1152]{2,1,0:T(8,128)} fusion(pred[512,1152]{1,0:T(8,128)(4,1)S(1)} %fusion.21, bf16[512,8,128]{2,0,1:T(8,128)(2,1)S(1)} %copy.30, bf16[512,8,128]{2,0,1:T(8,128)(2,1)} %bitcast.103, bf16[128,8,128]{2,0,1:T(8,128)(2,1)S(1)} %copy.28, bf16[512,8,128]{2,1,0:T(8,128)(2,1)S(1)} %bitcast.102), kind=kOutput, calls=%fused_computation.4 | convolution fusion | flops 1224474624 | bytes 22872064 | tf_op jit(solution)/shard_map/thd,nhd->htn/dot_general | solution.py:49
  432.6 15.6 %exponential_reduce_fusion = f32[8,512]{1,0:T(8,128)S(1)} fusion(f32[8,512,1152]{2,1,0:T(8,128)} %fusion.2), kind=kOutput, calls=%fused_computation.6 | output fusion | flops 9438335 | bytes 18890752 | tf_op jit(solution)/shard_map/sub | solution.py:58
  448.3 21.1 %fusion.29 = bf16[8,128,512]{2,1,0:T(8,128)(2,1)} fusion(f32[8,512]{1,0:T(8,128)S(1)} %exponential_reduce_fusion, bf16[512,8,128]{0,2,1:T(8,128)(2,1)S(1)} %bitcast.106, bf16[512,8,128]{0,2,1:T(8,128)(2,1)} %copy.25, bf16[128,8,128]{0,2,1:T(8,128)(2,1)S(1)} %bitcast.109, f32[8,512,1152]{2,1,0:T(8,128)} %fusion.2), kind=kOutput, calls=%fused_computation.47 | convolution fusion | flops 1229722752 | bytes 22298624 | tf_op jit(solution)/shard_map/htn,nhd->thd/dot_general | solution.py:60
  469.4 2.5 copy.34
  471.9 108.0 %reduce-scatter.5.cloned.1.call-done = bf16[128,2,2048]{2,0,1:T(8,128)(2,1)} async-done(((bf16[2048,2,2048]{2,0,1:T(8,128)(2,1)}), bf16[128,2,2048]{2,0,1:T(8,128)(2,1)}) %reduce-scatter.5.cloned.1.call-update) | async-done | bytes 1048592 | tf_op jit(solution)/shard_map/reduce_scatter | solution.py:81
  579.9 4.4 multiply_add_fusion
  584.3 2.9 copy.35
  587.3 2.9 copy.36
  (80 shorter events, 32.5 us)
Async XLA Ops:
  7.2 1.6 copy-start
  7.2 51.6 %all-gather.13.cloned.1.call-start = ((), (), s32[]{:S(2)}) async-start(), calls=%async_computation.7 | async-start | bytes 3145728 | tf_op jit(solution)/shard_map/all_gather | solution.py:118
  18.5 1.6 copy-start.3
  22.8 70.6 %all-gather.11.cloned.1.call-start = ((), (), s32[]{:S(2)}) async-start(), calls=%async_computation.6 | async-start | bytes 3145728 | tf_op jit(solution)/shard_map/all_gather | solution.py:117
  23.5 198.6 %all-gather.7.cloned.1.call-start = ((), (), s32[]{:S(2)}) async-start(), calls=%async_computation.2 | async-start | bytes 17825792 | tf_op jit(solution)/shard_map/all_gather | solution.py:107
  27.3 275.5 %reduce-scatter.3.cloned.1.call-start = ((), (), s32[]{:S(2)}) async-start(), calls=%async_computation.3 | async-start | bytes 6291456 | tf_op jit(solution)/shard_map/reduce_scatter | solution.py:120
  222.1 16.0 %copy-start.11 = (bf16[2048,2,2048]{2,0,1:T(8,128)(2,1)S(1)}, bf16[2048,2,2048]{2,0,1:T(8,128)(2,1)}, u32[]{:S(2)}) copy-start(bf16[2048,2,2048]{2,0,1:T(8,128)(2,1)} %all-gather.7.cloned.1.call-done) | copy-start | bytes 50331652
  250.1 55.7 %copy-start.12 = (u32[32]{0:T(128)S(1)}, u32[32]{0:T(128)}, u32[]{:S(2)}) copy-start(u32[32]{0:T(128)} %constant.85) | copy-start | bytes 388
  250.1 56.4 %copy-start.10 = (f32[1,512]{1,0:T(1,128)S(1)}, f32[1,512]{1,0:T(1,128)}, u32[]{:S(2)}) copy-start(f32[1,512]{1,0:T(1,128)} %param.15) | copy-start | bytes 6148
  250.1 114.2 %copy-start.9 = (f32[2048]{0:T(1024)S(1)}, f32[2048]{0:T(1024)}, u32[]{:S(2)}) copy-start(f32[2048]{0:T(1024)} %param.14) | copy-start | bytes 24580
  250.1 116.6 %all-gather.9.cloned.1.call-start = ((), (), s32[]{:S(2)}) async-start(), calls=%async_computation.4 | async-start | bytes 3145728 | tf_op jit(solution)/shard_map/all_gather | solution.py:125
  305.8 274.2 %reduce-scatter.5.cloned.1.call-start = ((), (), s32[]{:S(2)}) async-start(), calls=%async_computation.5 | async-start | bytes 17825792 | tf_op jit(solution)/shard_map/reduce_scatter | solution.py:81
  406.2 1.9 copy-start.5
  406.3 2.1 copy-start.7
  407.7 3.5 copy-start.4
  432.6 15.6 %copy-start.6 = (bf16[512,1,1024]{0,2,1:T(8,128)(2,1)S(1)}, bf16[512,1,1024]{0,2,1:T(8,128)(2,1)}, u32[]{:S(2)}) copy-start(bf16[512,1,1024]{0,2,1:T(8,128)(2,1)} %copy.37) | copy-start | bytes 3145732
  432.6 15.6 %copy-start.8 = (bf16[1,128,1024]{1,2,0:T(8,128)(2,1)S(1)}, bf16[1,128,1024]{1,2,0:T(8,128)(2,1)}, u32[]{:S(2)}) copy-start(bf16[1,128,1024]{1,2,0:T(8,128)(2,1)} %copy.23) | copy-start | bytes 786436
  448.3 131.7 %copy-start.2 = (f32[128,2,2048]{2,1,0:T(2,128)S(1)}, f32[128,2,2048]{2,1,0:T(2,128)}, u32[]{:S(2)}) copy-start(f32[128,2,2048]{2,1,0:T(2,128)} %param.18) | copy-start | bytes 6291460
  584.3 5.9 copy-start.1
Sparse Core Ops, SparseCore 0:
  22.9 35.8 all-gather.12
  60.3 33.0 all-gather.10
  95.6 126.4 all-gather.6
  250.3 52.5 reduce-scatter.2
  305.9 33.0 all-gather.8
  406.4 173.5 reduce-scatter.4
where the time goes:
time: 606 us; the launch traced here: 597 us
  waiting for transfers between devices  356 us (59%)
  matrix products  97.2 us (16%)
  local copies, waits for them, and re-layouts  44.4 us (7%)
  other arithmetic  38.7 us (6%)
  blocking collectives  33 us (5%)
  between operations  16 us (3%)
  loops' own time  11.6 us (2%)
    all_gather x1, waiting for transfers between devices, on_device(): lax.all_gather(memory.astype(jnp.bfloat16), 'seq', axis=0, tiled=True)  129 us
    reduce_scatter x1, waiting for transfers between devices, reduce_terms(): lax.psum_scatter(jnp.stack([grad_first, grad_second], axis=1).astype(jnp....  108 us
    reduce_scatter x1, waiting for transfers between devices, on_device(): lax.psum_scatter(partial_out.astype(jnp.bfloat16), 'head', scatter_dimens...  52.2 us
    all_gather x1, waiting for transfers between devices, on_device(): query_full = lax.all_gather(query, 'head', axis=1, tiled=True)  34.7 us
    unnamed x1, blocking collectives  33 us
    all_gather x1, waiting for transfers between devices, on_device(): keys_full = lax.all_gather(keys, 'head', axis=1, tiled=True)  31.4 us
    unnamed x38, local copies, waits for them, and re-layouts  21.8 us
    dot_general x1, matrix products, attend_local(): jnp.einsum('htn,nhd->thd', probs, all_values, preferred_element_type=jnp....  21.1 us
  transfers between devices with their start and end apart: 6, of which 5 were waited for; matrix products, arithmetic and copies ran while one was open for 14% of the time, Pallas kernels for 0%

commit v1 on v0

--- a/solution.py
+++ b/solution.py
@@ -115,7 +115,7 @@
     keys = proj[:, 1]
     values = proj[:, 2]
     query_full = lax.all_gather(query, "head", axis=1, tiled=True)
-    keys_full = lax.all_gather(keys, "head", axis=1, tiled=True)
+    keys_full = jnp.concatenate(lax.all_gather(keys, "head"), axis=1)
     preact, hidden, partial_out = memory_forward(query_full, keys_full, first, second)
     summed = lax.psum_scatter(
         partial_out.astype(jnp.bfloat16), "head", scatter_dimension=1, tiled=True

time: 606 us -> 600 us (0.990)
    unnamed x38 -> x40, local copies, waits for them, and re-layouts: 21.8 us -> 22 us
  transfers between devices with their start and end apart: 6 -> 6, of which waited for: 5 -> 5; matrix products, arithmetic and copies ran while one was open for 14% -> 15% of each run, Pallas kernels for 0% -> 0%
where the time goes in v1:
time: 600 us; the launch traced here: 596 us
  waiting for transfers between devices  353 us (59%)
  matrix products  96.7 us (16%)
  local copies, waits for them, and re-layouts  46.7 us (8%)
  other arithmetic  38.8 us (6%)
  blocking collectives  33.5 us (6%)
  between operations  16 us (3%)
  loops' own time  10.7 us (2%)
    all_gather x1, waiting for transfers between devices, on_device(): lax.all_gather(memory.astype(jnp.bfloat16), 'seq', axis=0, tiled=True)  129 us
    reduce_scatter x1, waiting for transfers between devices, reduce_terms(): lax.psum_scatter(jnp.stack([grad_first, grad_second], axis=1).astype(jnp....  108 us
    reduce_scatter x1, waiting for transfers between devices, on_device(): lax.psum_scatter(partial_out.astype(jnp.bfloat16), 'head', scatter_dimens...  52.6 us
    unnamed x1, blocking collectives  33.5 us
    all_gather x1, waiting for transfers between devices, on_device(): query_full = lax.all_gather(query, 'head', axis=1, tiled=True)  31.5 us
    all_gather x1, waiting for transfers between devices, on_device(): keys_full = jnp.concatenate(lax.all_gather(keys, 'head'), axis=1)  31.1 us
    unnamed x40, local copies, waits for them, and re-layouts  22 us
    dot_general x1, matrix products, attend_local(): jnp.einsum('htn,nhd->thd', probs, all_values, preferred_element_type=jnp....  21.1 us
  transfers between devices with their start and end apart: 6, of which 5 were waited for; matrix products, arithmetic and copies ran while one was open for 15% of the time, Pallas kernels for 0%

profile of v1, /device:TPU:0, one launch (start us, length us, event | category | flops | bytes accessed | tf_op | source)
XLA Modules:
  0.0 595.8 jit_solution(4973615449533981255)
XLA Ops:
  8.8 9.8 %convolution_convert_fusion = bf16[512,3,1024]{2,0,1:T(8,128)(2,1)S(1)} fusion(bf16[2048,3,1024]{2,0,1:T(8,128)(2,1)} %param.12, bf16[1,512,2048]{2,1,0:T(8,128)(2,1)S(1)} %copy-done), kind=kOutput, calls=%fused_computation.35 | convolution fusion | flops 6444023808 | bytes 17825792 | tf_op jit(solution)/shard_map/td,dkf->tkf/dot_general | solution.py:111
  20.3 2.6 fusion.44
  23.7 3.7 copy.54
  27.8 31.1 %all-gather.13.cloned.1.call-done = bf16[1024,1,1024]{2,0,1:T(8,128)(2,1)} async-done(((bf16[512,1,1024]{2,0,1:T(8,128)(2,1)}), bf16[1024,1,1024]{2,0,1:T(8,128)(2,1)}) %all-gather.13.cloned.1.call-update) | async-done | bytes 2097168 | tf_op jit(solution)/shard_map/all_gather | solution.py:118
  58.9 3.2 copy.42
  62.0 31.5 %all-gather.11.cloned.1.call-done = bf16[512,1,2048]{2,0,1:T(8,128)(2,1)} async-done(((bf16[512,1,1024]{2,0,1:T(8,128)(2,1)}), bf16[512,1,2048]{2,0,1:T(8,128)(2,1)}) %all-gather.11.cloned.1.call-update) | async-done | bytes 2097168 | tf_op jit(solution)/shard_map/all_gather | solution.py:117
  93.6 128.7 %all-gather.7.cloned.1.call-done = bf16[2048,2,2048]{2,0,1:T(8,128)(2,1)} async-done(((bf16[128,2,2048]{2,0,1:T(8,128)(2,1)}), bf16[2048,2,2048]{2,0,1:T(8,128)(2,1)}) %all-gather.7.cloned.1.call-update) | async-done | bytes 16777232 | tf_op jit(solution)/shard_map/all_gather | solution.py:107
  222.2 16.0 %multiply_convert_fusion = (bf16[1024,2048]{1,0:T(8,128)(2,1)}, f32[1024,2048]{1,0:T(8,128)}) fusion(bf16[2048,2,2048]{2,0,1:T(8,128)(2,1)} %all-gather.7.cloned.1.call-done, bf16[512,2048]{1,0:T(8,128)(2,1)} %bitcast.109, bf16[512,2048]{1,0:T(8,128)(2,1)} %bitcast.121), kind=kOutput, calls=%fused_computation.14 | convolution fusion | flops 8608808960 | bytes 25165824 | tf_op jit(solution)/shard_map/dot_general | solution.py:66
  238.3 12.0 %fusion.10 = bf16[1024,2048]{1,0:T(8,128)(2,1)} fusion(bf16[1024,2048]{1,0:T(8,128)(2,1)} %get-tuple-element.139, bf16[2048,2,2048]{2,0,1:T(8,128)(2,1)S(1)} %copy-done.12), kind=kOutput, calls=%fused_computation.22 | convolution fusion | flops 8592031744 | bytes 16777216 | tf_op jit(solution)/shard_map/dot_general | solution.py:68
  250.4 52.6 %reduce-scatter.3.cloned.1.call-done = bf16[1024,1024]{1,0:T(8,128)(2,1)} async-done(((bf16[1024,2048]{1,0:T(8,128)(2,1)}), bf16[1024,1024]{1,0:T(8,128)(2,1)}) %reduce-scatter.3.cloned.1.call-update) | async-done | bytes 2097168 | tf_op jit(solution)/shard_map/reduce_scatter | solution.py:120
  303.0 2.9 fusion.23
  308.6 33.5 %all-reduce = f32[16]{0:T(128)S(1)} all-reduce(f32[16]{0:T(128)S(1)} %dynamic-update-slice), channel_id=1, replica_groups=mesh['seq'=16,'head'=2] {'seq'}, use_global_device_ids=true, to_apply=%add | all-reduce | flops 16 | bytes 128
  342.8 20.5 %while.15 = (s32[]{:T(128)}, f32[1]{0:T(128)}, s32[]{:T(128)}, f32[16,1]{0,1:T(1,128)S(1)}, s32[]{:T(128)}, /*index=5*/s32[]{:T(128)}, s32[]{:T(128)}, s32[]{:T(128)}) while((s32[]{:T(128)}, f32[1]{0:T(128)}, s32[]{:T(128)}, f32[16,1]{0,1:T(1,128)S(1)}, s32[]{:T(128)}, /*index=5*/s32[]{:T(128)}, s32[]{:T(128)}, s32[]{:T(128)}) %tuple.65), condition=%wide.region_7.8_spmd, body=%wide.region_6.7_spmd.sunk | while | flops 9 | bytes 177 | solution.py:20
  365.8 10.2 %convert_bitcast_fusion = bf16[2048,1,2048]{2,0,1:T(8,128)(2,1)} fusion(bf16[512,2048]{1,0:T(8,128)(2,1)} %all-gather.9.cloned.1.call-done, bf16[1024,2048]{1,0:T(8,128)(2,1)} %get-tuple-element.139, f32[512]{0:T(512)S(1)} %fusion.38), kind=kOutput, calls=%fused_computation.12 | convolution fusion | flops 4302307328 | bytes 12584960 | tf_op jit(solution)/shard_map/dot_general | solution.py:78
  376.1 14.9 %convert_bitcast_fusion.1 = bf16[2048,1,2048]{2,0,1:T(8,128)(2,1)} fusion(bf16[512,2048]{1,0:T(8,128)(2,1)S(1)} %bitcast.110, f32[1024,2048]{1,0:T(8,128)} %get-tuple-element.140, bf16[512,2048]{1,0:T(8,128)(2,1)} %all-gather.9.cloned.1.call-done, bf16[2048,2,2048]{2,0,1:T(8,128)(2,1)} %all-gather.7.cloned.1.call-done, f32[512]{0:T(512)S(1)} %fusion.38), kind=kOutput, calls=%fused_computation.13 | convolution fusion | flops 8604614656 | bytes 25167872 | tf_op jit(solution)/shard_map/dot_general | solution.py:75
  391.0 13.8 %pad_maximum_fusion = bf16[2048,2,2048]{2,0,1:T(8,128)(2,1)} fusion(bf16[2048,1,2048]{2,0,1:T(8,128)(2,1)} %convert_bitcast_fusion, bf16[2048,1,2048]{2,0,1:T(8,128)(2,1)} %convert_bitcast_fusion.1), kind=kLoop, calls=%fused_computation.7 | loop fusion | flops 8388608 | bytes 33554432 | tf_op jit(solution)/shard_map/stack | solution.py:82
  420.3 10.9 %fusion.2 = f32[8,512,1152]{2,1,0:T(8,128)} fusion(pred[512,1152]{1,0:T(8,128)(4,1)S(1)} %fusion.21, bf16[512,8,128]{2,0,1:T(8,128)(2,1)S(1)} %copy.32, bf16[512,8,128]{2,0,1:T(8,128)(2,1)} %bitcast.106, bf16[128,8,128]{2,0,1:T(8,128)(2,1)S(1)} %copy.30, bf16[512,8,128]{2,1,0:T(8,128)(2,1)S(1)} %bitcast.105), kind=kOutput, calls=%fused_computation.4 | convolution fusion | flops 1224474624 | bytes 22872064 | tf_op jit(solution)/shard_map/thd,nhd->htn/dot_general | solution.py:49
  431.2 15.6 %exponential_reduce_fusion = f32[8,512]{1,0:T(8,128)S(1)} fusion(f32[8,512,1152]{2,1,0:T(8,128)} %fusion.2), kind=kOutput, calls=%fused_computation.6 | output fusion | flops 9438335 | bytes 18890752 | tf_op jit(solution)/shard_map/sub | solution.py:58
  446.8 21.1 %fusion.29 = bf16[8,128,512]{2,1,0:T(8,128)(2,1)} fusion(f32[8,512]{1,0:T(8,128)S(1)} %exponential_reduce_fusion, bf16[512,8,128]{0,2,1:T(8,128)(2,1)S(1)} %bitcast.112, bf16[512,8,128]{0,2,1:T(8,128)(2,1)} %copy.27, bf16[128,8,128]{0,2,1:T(8,128)(2,1)S(1)} %bitcast.115, f32[8,512,1152]{2,1,0:T(8,128)} %fusion.2), kind=kOutput, calls=%fused_computation.47 | convolution fusion | flops 1229722752 | bytes 22298624 | tf_op jit(solution)/shard_map/htn,nhd->thd/dot_general | solution.py:60
  467.9 2.5 copy.36
  470.4 108.0 %reduce-scatter.5.cloned.1.call-done = bf16[128,2,2048]{2,0,1:T(8,128)(2,1)} async-done(((bf16[2048,2,2048]{2,0,1:T(8,128)(2,1)}), bf16[128,2,2048]{2,0,1:T(8,128)(2,1)}) %reduce-scatter.5.cloned.1.call-update) | async-done | bytes 1048592 | tf_op jit(solution)/shard_map/reduce_scatter | solution.py:81
  578.5 4.4 multiply_add_fusion
  582.8 2.9 copy.37
  585.8 2.9 copy.38
  (83 shorter events, 34.2 us)
Async XLA Ops:
  7.2 1.6 copy-start
  7.2 51.7 %all-gather.13.cloned.1.call-start = ((), (), s32[]{:S(2)}) async-start(), calls=%async_computation.7 | async-start | bytes 3145728 | tf_op jit(solution)/shard_map/all_gather | solution.py:118
  18.5 1.8 copy-start.3
  22.9 70.6 %all-gather.11.cloned.1.call-start = ((), (), s32[]{:S(2)}) async-start(), calls=%async_computation.6 | async-start | bytes 3145728 | tf_op jit(solution)/shard_map/all_gather | solution.py:117
  23.7 198.6 %all-gather.7.cloned.1.call-start = ((), (), s32[]{:S(2)}) async-start(), calls=%async_computation.2 | async-start | bytes 17825792 | tf_op jit(solution)/shard_map/all_gather | solution.py:107
  27.5 275.5 %reduce-scatter.3.cloned.1.call-start = ((), (), s32[]{:S(2)}) async-start(), calls=%async_computation.3 | async-start | bytes 6291456 | tf_op jit(solution)/shard_map/reduce_scatter | solution.py:120
  222.2 16.0 %copy-start.12 = (bf16[2048,2,2048]{2,0,1:T(8,128)(2,1)S(1)}, bf16[2048,2,2048]{2,0,1:T(8,128)(2,1)}, u32[]{:S(2)}) copy-start(bf16[2048,2,2048]{2,0,1:T(8,128)(2,1)} %all-gather.7.cloned.1.call-done) | copy-start | bytes 50331652
  250.3 55.7 %copy-start.13 = (u32[32]{0:T(128)S(1)}, u32[32]{0:T(128)}, u32[]{:S(2)}) copy-start(u32[32]{0:T(128)} %constant.85) | copy-start | bytes 388
  250.3 56.4 %copy-start.11 = (f32[1,512]{1,0:T(1,128)S(1)}, f32[1,512]{1,0:T(1,128)}, u32[]{:S(2)}) copy-start(f32[1,512]{1,0:T(1,128)} %param.15) | copy-start | bytes 6148
  250.3 113.0 %copy-start.10 = (f32[2048]{0:T(1024)S(1)}, f32[2048]{0:T(1024)}, u32[]{:S(2)}) copy-start(f32[2048]{0:T(1024)} %param.14) | copy-start | bytes 24580
  250.3 115.5 %all-gather.9.cloned.1.call-start = ((), (), s32[]{:S(2)}) async-start(), calls=%async_computation.4 | async-start | bytes 3145728 | tf_op jit(solution)/shard_map/all_gather | solution.py:125
  306.0 272.5 %reduce-scatter.5.cloned.1.call-start = ((), (), s32[]{:S(2)}) async-start(), calls=%async_computation.5 | async-start | bytes 17825792 | tf_op jit(solution)/shard_map/reduce_scatter | solution.py:81
  365.8 10.3 %copy-start.6 = (bf16[2,64,8,1024]{3,2,0,1:T(8,128)(2,1)S(1)}, bf16[2,64,8,1024]{3,2,0,1:T(8,128)(2,1)}, u32[]{:S(2)}) copy-start(bf16[2,64,8,1024]{3,2,0,1:T(8,128)(2,1)} %copy.42) | copy-start | bytes 6291460
  404.8 1.9 copy-start.5
  404.8 2.1 copy-start.8
  406.2 3.5 copy-start.4
  431.2 15.6 %copy-start.7 = (bf16[512,1,1024]{0,2,1:T(8,128)(2,1)S(1)}, bf16[512,1,1024]{0,2,1:T(8,128)(2,1)}, u32[]{:S(2)}) copy-start(bf16[512,1,1024]{0,2,1:T(8,128)(2,1)} %copy.39) | copy-start | bytes 3145732
  431.2 15.6 %copy-start.9 = (bf16[1,128,1024]{1,2,0:T(8,128)(2,1)S(1)}, bf16[1,128,1024]{1,2,0:T(8,128)(2,1)}, u32[]{:S(2)}) copy-start(bf16[1,128,1024]{1,2,0:T(8,128)(2,1)} %copy.24) | copy-start | bytes 786436
  446.8 131.7 %copy-start.2 = (f32[128,2,2048]{2,1,0:T(2,128)S(1)}, f32[128,2,2048]{2,1,0:T(2,128)}, u32[]{:S(2)}) copy-start(f32[128,2,2048]{2,1,0:T(2,128)} %param.18) | copy-start | bytes 6291460
  582.8 5.9 copy-start.1
Sparse Core Ops, SparseCore 0:
  23.0 35.8 all-gather.12
  60.4 33.0 all-gather.10
  95.8 126.4 all-gather.6
  250.4 52.5 reduce-scatter.2
  306.1 33.1 all-gather.8
  404.9 173.5 reduce-scatter.4
